TPU v7x, 32 devices: a whole 2x2x4 slice. The times are simulated.
32 devices in a mesh: row: 4 (over x, core), col: 8 (over z, y).
Axes of the slice: x: 2, y: 2, z: 4, core: 2. Of those that a mesh axis runs over, the one named last changes fastest.
Arguments:
- ancestor_inverse: bfloat16 [24576, 24576], P('row', 'col'), may hold values from -0.0390625 to 0.0390625
- panels: bfloat16 [24576, 3, 512], P(('row', 'col')), may hold values from -1.1953125 to 1.1953125
- diag_inverse: float32 [3, 512, 512], replicated, may hold values from -6 to 6
- tile_mask: int32 [3, 192], replicated, may hold values 0 or 1
Outputs:
- off_diagonal: float32 [24576, 3, 512], P(('row', 'col'))
- diagonal: float32 [3, 512, 512], replicated
All inputs are finite; a program needn't handle non-finite values.
Results may differ from a plain program's by a relative error of at most 0.0003.
Values may be sent and summed in bfloat16 or wider, within the bound.
A program may use at most 192 MiB of HBM per device.

v0:
```python
import jax
import jax.numpy as jnp
from jax import lax
from jax.sharding import PartitionSpec as P


def exchange(partial, axis):
    count = lax.axis_size(axis)
    rows, width = partial.shape
    return lax.psum_scatter(partial, axis, scatter_dimension=0, tiled=True)


def body(ancestor_inverse, panels, diag_inverse, tile_mask):
    row_count = lax.axis_size("row")
    col_count = lax.axis_size("col")
    span = lax.axis_index("row") * col_count + lax.axis_index("col")
    kept_rows = panels.shape[0]
    panel_count = panels.shape[1]
    tile = kept_rows * row_count * col_count // tile_mask.shape[1]
    full_mask = jnp.repeat(tile_mask, tile, axis=1).astype(jnp.bfloat16)
    own_mask = lax.dynamic_slice_in_dim(full_mask, span * kept_rows, kept_rows, 1)
    moves = [
        (index, index % row_count * col_count + index // row_count)
        for index in range(row_count * col_count)
    ]
    masked = [panels[:, p, :] * own_mask[p][:, None] for p in range(panel_count)]
    sent = [lax.ppermute(block, ("row", "col"), moves) for block in masked]
    sides = [lax.all_gather(block, "row", axis=0, tiled=True) for block in sent]
    results, parts = ([], [])
    for p in range(panel_count):
        partial = jnp.dot(ancestor_inverse, sides[p], preferred_element_type=jnp.float32)
        summed = -exchange(partial, "col")
        results.append(summed)
        parts.append(
            lax.dot_general(
                masked[p].astype(jnp.float32),
                summed,
                (((0,), (0,)), ((), ())),
                precision=lax.Precision.HIGHEST,
            )
        )
    off_diagonal = jnp.stack(results, axis=1)
    schur = lax.psum(jnp.stack(parts), ("row", "col"))
    return (off_diagonal, diag_inverse - schur)


def solution(mesh):
    return jax.shard_map(
        body,
        mesh=mesh,
        in_specs=(P("row", "col"), P(("row", "col"), None, None), P(), P()),
        out_specs=(P(("row", "col"), None, None), P()),
        check_vma=False,
    )
```

profile of v0, /device:TPU:0, one launch (start us, length us, event | category | flops | bytes accessed | tf_op | source)
XLA Modules:
  0.0 952.1 jit_solution(13903537531053839367)
XLA Ops:
  7.2 0.7 convert_element_type.10
  7.9 0.1 broadcast_bitcast_fusion
  8.1 0.1 copy.9
  8.2 0.1 dynamic-slice_reduce_fusion.2
  8.3 2.0 bitcast_multiply_fusion.2
  10.3 1.6 collective-permute-start.2
  12.0 1.6 collective-permute-start
  13.6 1.5 collective-permute-start.1
  15.2 86.4 %all-gather.8.cloned.1.call-done = bf16[3072,512]{1,0:T(8,128)(2,1)} async-done(((bf16[768,512]{1,0:T(8,128)(2,1)}), bf16[3072,512]{1,0:T(8,128)(2,1)}) %all-gather.8.cloned.1.call-update) | async-done | bytes 3145744 | tf_op jit(solution)/shard_map/all_gather | solution.py:28
  101.6 27.8 %convolution_bitcast_fusion = f32[6144,512]{0,1:T(8,128)} fusion(bf16[3072,512]{1,0:T(8,128)(2,1)} %all-gather.8.cloned.1.call-done, bf16[6144,3072]{1,0:T(8,128)(2,1)} %param.4), kind=kOutput, calls=%fused_computation | convolution fusion | flops 19327352832 | bytes 53477376 | tf_op jit(solution)/shard_map/dot_general | solution.py:31
  129.4 0.2 reduce-scatter.4.cloned.1.call-start
  129.7 5.6 all-gather.4.cloned.1.call-done
  135.3 27.7 %convolution_bitcast_fusion.2 = f32[6144,512]{0,1:T(8,128)} fusion(bf16[3072,512]{1,0:T(8,128)(2,1)} %all-gather.4.cloned.1.call-done, bf16[6144,3072]{1,0:T(8,128)(2,1)} %param.4), kind=kOutput, calls=%fused_computation.2 | convolution fusion | flops 19327352832 | bytes 53477376 | tf_op jit(solution)/shard_map/dot_general | solution.py:31
  163.1 0.3 reduce-scatter.6.cloned.1.call-start
  163.3 3.3 all-gather.6.cloned.1.call-done
  166.6 27.7 %convolution_bitcast_fusion.1 = f32[6144,512]{0,1:T(8,128)} fusion(bf16[3072,512]{1,0:T(8,128)(2,1)} %all-gather.6.cloned.1.call-done, bf16[6144,3072]{1,0:T(8,128)(2,1)} %param.4), kind=kOutput, calls=%fused_computation.1 | convolution fusion | flops 19327352832 | bytes 53477376 | tf_op jit(solution)/shard_map/dot_general | solution.py:31
  194.3 0.3 all-reduce.2.cloned.1.call-start
  194.6 182.9 %reduce-scatter.8.cloned.1.call-done = f32[768,512]{0,1:T(8,128)} async-done(((f32[6144,512]{0,1:T(8,128)}), f32[768,512]{0,1:T(8,128)}) %reduce-scatter.8.cloned.1.call-update) | async-done | bytes 1572880 | tf_op jit(solution)/shard_map/reduce_scatter | solution.py:10
  377.5 3.1 fusion.12
  380.7 206.9 %reduce-scatter.4.cloned.1.call-done = f32[768,512]{0,1:T(8,128)} async-done(((f32[6144,512]{0,1:T(8,128)}), f32[768,512]{0,1:T(8,128)}) %reduce-scatter.4.cloned.1.call-update) | async-done | bytes 1572880 | tf_op jit(solution)/shard_map/reduce_scatter | solution.py:10
  587.6 3.4 fusion.6
  590.9 206.7 %reduce-scatter.6.cloned.1.call-done = f32[768,512]{0,1:T(8,128)} async-done(((f32[6144,512]{0,1:T(8,128)}), f32[768,512]{0,1:T(8,128)}) %reduce-scatter.6.cloned.1.call-update) | async-done | bytes 1572880 | tf_op jit(solution)/shard_map/reduce_scatter | solution.py:10
  797.6 3.1 fusion.9
  800.7 2.0 pad_maximum_fusion.1
  802.7 1.4 copy-done
  804.1 0.1 negate_bitcast_fusion
  804.2 0.4 copy-done.2
  804.7 0.9 copy-done.1
  805.8 2.4 pad_maximum_fusion
  808.2 6.2 copy.6
  814.4 126.5 %all-reduce.2.cloned.1.call-done = f32[3,512,512]{2,1,0:T(8,128)} async-done(((f32[3,512,512]{2,1,0:T(8,128)}), f32[3,512,512]{2,1,0:T(8,128)}) %all-reduce.2.cloned.1.call-update) | async-done | bytes 3145744 | tf_op jit(solution)/shard_map/psum | solution.py:43
  941.0 4.3 sub.3
  (23 shorter events, 0.5 us)
Async XLA Ops:
  7.2 94.5 %all-gather.8.cloned.1.call-start = ((), (), s32[]{:S(2)}) async-start(), calls=%async_computation.7 | async-start | bytes 3932160 | tf_op jit(solution)/shard_map/all_gather | solution.py:28
  10.3 119.1 %copy-start.4 = (bf16[768,512]{1,0:T(8,128)(2,1)}, bf16[768,512]{1,0:T(8,128)(2,1)S(1)}, u32[]{:S(2)}) copy-start(bf16[768,512]{1,0:T(8,128)(2,1)S(1)} %get-tuple-element.7) | copy-start | bytes 2359300
  10.3 1.6 collective-permute-start.2
  11.9 123.4 %all-gather.4.cloned.1.call-start = ((), (), s32[]{:S(2)}) async-start(), calls=%async_computation.3 | async-start | bytes 3932160 | tf_op jit(solution)/shard_map/all_gather | solution.py:28
  12.0 1.6 collective-permute-start
  13.6 153.1 %all-gather.6.cloned.1.call-start = ((), (), s32[]{:S(2)}) async-start(), calls=%async_computation.5 | async-start | bytes 3932160 | tf_op jit(solution)/shard_map/all_gather | solution.py:28
  13.6 1.5 collective-permute-start.1
  15.2 362.4 %reduce-scatter.8.cloned.1.call-start = ((), (), s32[]{:S(2)}) async-start(), calls=%async_computation.8 | async-start | bytes 14155776 | tf_op jit(solution)/shard_map/reduce_scatter | solution.py:10
  129.4 458.1 %reduce-scatter.4.cloned.1.call-start = ((), (), s32[]{:S(2)}) async-start(), calls=%async_computation.4 | async-start | bytes 14155776 | tf_op jit(solution)/shard_map/reduce_scatter | solution.py:10
  163.1 634.6 %reduce-scatter.6.cloned.1.call-start = ((), (), s32[]{:S(2)}) async-start(), calls=%async_computation.6 | async-start | bytes 14155776 | tf_op jit(solution)/shard_map/reduce_scatter | solution.py:10
  194.3 746.7 %all-reduce.2.cloned.1.call-start = ((), (), s32[]{:S(2)}) async-start(), calls=%async_computation.9 | async-start | bytes 6291456 | tf_op jit(solution)/shard_map/psum | solution.py:43
  802.7 1.4 copy-start
  802.7 1.9 copy-start.2
  804.1 1.5 copy-start.1
  808.2 132.8 %copy-start.3 = (f32[3,512,512]{2,1,0:T(8,128)S(1)}, f32[3,512,512]{2,1,0:T(8,128)}, u32[]{:S(2)}) copy-start(f32[3,512,512]{2,1,0:T(8,128)} %param.6) | copy-start | bytes 9437188
Sparse Core Ops, SparseCore 0:
  12.0 89.5 all-gather.7
  103.2 32.0 all-gather.3
  136.9 29.7 all-gather.5
  170.0 207.4 reduce-scatter.7
  381.0 206.5 reduce-scatter.3
  591.0 206.5 reduce-scatter.5
  803.7 137.2 all-reduce.1
where the time goes:
time: 953 us; the launch traced here: 952 us
  waiting for transfers between devices  818 us (86%)
  matrix products  92.8 us (10%)
  between operations  14.2 us (1%)
  other arithmetic  11.7 us (1%)
    reduce_scatter x3, waiting for transfers between devices, exchange(): return lax.psum_scatter(partial, axis, scatter_dimension=0, tiled=True)  597 us
    psum x1, waiting for transfers between devices, body(): schur = lax.psum(jnp.stack(parts), ('row', 'col'))  127 us
    all_gather x3, waiting for transfers between devices, body(): sides = [lax.all_gather(block, 'row', axis=0, tiled=True) for block in sent]  95.3 us
    dot_general x3, matrix products, body(): jnp.dot(ancestor_inverse, sides[p], preferred_element_type=jnp.float32)  83.2 us
  transfers between devices with their start and end apart: 10, of which 7 were waited for; matrix products, arithmetic and copies ran while one was open for 10% of the time, Pallas kernels for 0%

commit v1 on v0

--- a/solution.py
+++ b/solution.py
@@ -2,6 +2,11 @@
 import jax.numpy as jnp
 from jax import lax
 from jax.sharding import PartitionSpec as P
+
+
+def exchange_gather(shard, name, dim):
+    stack = jnp.stack([shard] * lax.axis_size(name))
+    return jnp.concatenate(lax.all_to_all(stack, name, 0, 0), axis=dim)
 
 
 def exchange(partial, axis):
@@ -25,7 +30,7 @@
     ]
     masked = [panels[:, p, :] * own_mask[p][:, None] for p in range(panel_count)]
     sent = [lax.ppermute(block, ("row", "col"), moves) for block in masked]
-    sides = [lax.all_gather(block, "row", axis=0, tiled=True) for block in sent]
+    sides = [exchange_gather(block, "row", 0) for block in sent]
     results, parts = ([], [])
     for p in range(panel_count):
         partial = jnp.dot(ancestor_inverse, sides[p], preferred_element_type=jnp.float32)

time: 953 us -> 943 us (0.990)
  waiting for transfers between devices: 818 us -> 540 us
  blocking collectives: 0 us -> 270 us
    all_to_all x0 -> x3, blocking collectives: none -> 270 us  [exchange_gather(): return jnp.concatenate(lax.all_to_all(stack, name, 0, 0), axis=dim)]
    reduce_scatter x3, waiting for transfers between devices: 597 us -> 414 us  [exchange(): return lax.psum_scatter(partial, axis, scatter_dimension=0, tiled=True)]
    all_gather x3 -> x0, waiting for transfers between devices: 95.3 us -> none  [body(): sides = [lax.all_gather(block, 'row', axis=0, tiled=True) for block in sent]]
  transfers between devices with their start and end apart: 10 -> 7, of which waited for: 7 -> 4; matrix products, arithmetic and copies ran while one was open for 10% -> 7% of each run, Pallas kernels for 0% -> 0%
where the time goes in v1:
time: 943 us; the launch traced here: 942 us
  waiting for transfers between devices  540 us (57%)
  blocking collectives  270 us (29%)
  matrix products  90.1 us (10%)
  between operations  13.9 us (1%)
  other arithmetic  12.8 us (1%)
  local copies, waits for them, and re-layouts  12.8 us (1%)
    reduce_scatter x3, waiting for transfers between devices, exchange(): return lax.psum_scatter(partial, axis, scatter_dimension=0, tiled=True)  414 us
    all_to_all x3, blocking collectives, exchange_gather(): return jnp.concatenate(lax.all_to_all(stack, name, 0, 0), axis=dim)  270 us
    psum x1, waiting for transfers between devices, body(): schur = lax.psum(jnp.stack(parts), ('row', 'col'))  126 us
    dot_general x3, matrix products, body(): jnp.dot(ancestor_inverse, sides[p], preferred_element_type=jnp.float32)  80.5 us
  transfers between devices with their start and end apart: 7, of which 4 were waited for; matrix products, arithmetic and copies ran while one was open for 7% of the time, Pallas kernels for 0%

profile of v1, /device:TPU:0, one launch (start us, length us, event | category | flops | bytes accessed | tf_op | source)
XLA Modules:
  0.0 942.0 jit_solution(18227195926967831798)
XLA Ops:
  7.2 0.7 convert_element_type.10
  8.3 3.1 bitcast_multiply_fusion.2
  11.4 0.7 collective-permute-start.2
  12.3 0.2 stack.49
  12.6 62.3 %all_to_all.15 = bf16[4,768,512]{2,1,0:T(8,128)(2,1)S(1)} all-to-all(bf16[4,768,512]{2,1,0:T(8,128)(2,1)S(1)} %stack.49), channel_id=1, replica_groups=mesh['row'=4,'col'=8] {'row'}, dimensions={0} | all-to-all | bytes 6291456 | tf_op jit(solution)/shard_map/all_to_all | solution.py:9
  74.8 26.7 %convolution_bitcast_fusion = f32[6144,512]{0,1:T(8,128)} fusion(bf16[3072,512]{1,0:T(8,128)(2,1)S(1)} %bitcast.41, bf16[6144,3072]{1,0:T(8,128)(2,1)} %param.4), kind=kOutput, calls=%fused_computation | convolution fusion | flops 19327352832 | bytes 53477376 | tf_op jit(solution)/shard_map/dot_general | solution.py:36
  101.6 1.1 copy-done.6
  102.7 0.7 collective-permute-start
  103.4 0.2 stack.22
  103.6 95.1 %all_to_all.16 = bf16[4,768,512]{2,1,0:T(8,128)(2,1)S(1)} all-to-all(bf16[4,768,512]{2,1,0:T(8,128)(2,1)S(1)} %stack.22), channel_id=1, replica_groups=mesh['row'=4,'col'=8] {'row'}, dimensions={0} | all-to-all | bytes 6291456 | tf_op jit(solution)/shard_map/all_to_all | solution.py:9
  198.7 26.9 %convolution_bitcast_fusion.2 = f32[6144,512]{0,1:T(8,128)} fusion(bf16[3072,512]{1,0:T(8,128)(2,1)S(1)} %bitcast.42, bf16[6144,3072]{1,0:T(8,128)(2,1)} %param.4), kind=kOutput, calls=%fused_computation.2 | convolution fusion | flops 19327352832 | bytes 53477376 | tf_op jit(solution)/shard_map/dot_general | solution.py:36
  225.7 1.1 copy-done.4
  226.8 0.7 collective-permute-start.1
  227.5 0.2 stack.47
  227.8 112.4 %all_to_all.17 = bf16[4,768,512]{2,1,0:T(8,128)(2,1)S(1)} all-to-all(bf16[4,768,512]{2,1,0:T(8,128)(2,1)S(1)} %stack.47), channel_id=1, replica_groups=mesh['row'=4,'col'=8] {'row'}, dimensions={0} | all-to-all | bytes 6291456 | tf_op jit(solution)/shard_map/all_to_all | solution.py:9
  340.1 26.8 %convolution_bitcast_fusion.1 = f32[6144,512]{0,1:T(8,128)} fusion(bf16[3072,512]{1,0:T(8,128)(2,1)S(1)} %bitcast.43, bf16[6144,3072]{1,0:T(8,128)(2,1)} %param.4), kind=kOutput, calls=%fused_computation.1 | convolution fusion | flops 19327352832 | bytes 53477376 | tf_op jit(solution)/shard_map/dot_general | solution.py:36
  367.0 0.3 all-reduce.2.cloned.1.call-start
  367.3 0.3 reduce-scatter.8.cloned.1.call-done
  367.7 0.5 copy-done.8
  368.1 3.1 fusion.12
  371.2 206.6 %reduce-scatter.4.cloned.1.call-done = f32[768,512]{0,1:T(8,128)} async-done(((f32[6144,512]{0,1:T(8,128)}), f32[768,512]{0,1:T(8,128)}) %reduce-scatter.4.cloned.1.call-update) | async-done | bytes 1572880 | tf_op jit(solution)/shard_map/reduce_scatter | solution.py:15
  577.8 3.4 fusion.6
  581.2 206.8 %reduce-scatter.6.cloned.1.call-done = f32[768,512]{0,1:T(8,128)} async-done(((f32[6144,512]{0,1:T(8,128)}), f32[768,512]{0,1:T(8,128)}) %reduce-scatter.6.cloned.1.call-update) | async-done | bytes 1572880 | tf_op jit(solution)/shard_map/reduce_scatter | solution.py:15
  788.0 3.1 fusion.9
  791.1 2.0 pad_maximum_fusion.1
  793.1 1.4 copy-done
  794.6 0.4 copy-done.2
  795.1 0.9 copy-done.1
  796.1 2.4 pad_maximum_fusion
  798.6 6.2 copy.6
  804.8 126.4 %all-reduce.2.cloned.1.call-done = f32[3,512,512]{2,1,0:T(8,128)} async-done(((f32[3,512,512]{2,1,0:T(8,128)}), f32[3,512,512]{2,1,0:T(8,128)}) %all-reduce.2.cloned.1.call-update) | async-done | bytes 3145744 | tf_op jit(solution)/shard_map/psum | solution.py:48
  931.2 4.3 sub.3
  (28 shorter events, 1.1 us)
Async XLA Ops:
  7.2 360.5 %reduce-scatter.8.cloned.1.call-start = ((), (), s32[]{:S(2)}) async-start(), calls=%async_computation.8 | async-start | bytes 14155776 | tf_op jit(solution)/shard_map/reduce_scatter | solution.py:15
  11.4 0.9 copy-start.7
  11.4 0.9 collective-permute-start.2
  101.5 1.1 copy-start.6
  101.6 476.2 %reduce-scatter.4.cloned.1.call-start = ((), (), s32[]{:S(2)}) async-start(), calls=%async_computation.6 | async-start | bytes 14155776 | tf_op jit(solution)/shard_map/reduce_scatter | solution.py:15
  102.7 0.7 collective-permute-start
  225.7 1.1 copy-start.4
  225.7 562.3 %reduce-scatter.6.cloned.1.call-start = ((), (), s32[]{:S(2)}) async-start(), calls=%async_computation.7 | async-start | bytes 14155776 | tf_op jit(solution)/shard_map/reduce_scatter | solution.py:15
  226.8 0.7 collective-permute-start.1
  367.0 1.2 copy-start.8
  367.0 421.0 %copy-start.5 = (bf16[768,512]{1,0:T(8,128)(2,1)S(1)}, bf16[768,512]{1,0:T(8,128)(2,1)}, u32[]{:S(2)}) copy-start(bf16[768,512]{1,0:T(8,128)(2,1)} %get-tuple-element.9) | copy-start | bytes 2359300
  367.0 564.2 %all-reduce.2.cloned.1.call-start = ((), (), s32[]{:S(2)}) async-start(), calls=%async_computation.9 | async-start | bytes 6291456 | tf_op jit(solution)/shard_map/psum | solution.py:48
  793.1 1.4 copy-start
  793.1 1.9 copy-start.2
  794.5 1.5 copy-start.1
  798.6 132.6 %copy-start.3 = (f32[3,512,512]{2,1,0:T(8,128)S(1)}, f32[3,512,512]{2,1,0:T(8,128)}, u32[]{:S(2)}) copy-start(f32[3,512,512]{2,1,0:T(8,128)} %param.6) | copy-start | bytes 9437188
Sparse Core Ops, SparseCore 0:
  101.7 265.9 reduce-scatter.7
  371.2 206.5 reduce-scatter.3
  581.4 206.5 reduce-scatter.5
  793.9 137.2 all-reduce.1
